TPU v7x, 32 devices: a whole 2x2x4 slice. The times are simulated.
32 devices in a mesh: section: 4 (over y, x), cp: 4 (over z), tp: 2 (over core).
Axes of the slice: x: 2, y: 2, z: 4, core: 2. Of those that a mesh axis runs over, the one named last changes fastest.
Arguments:
- acts: bfloat16 [4, 512, 8192], P('section', 'cp', 'tp'), may hold values from -16 to 16
- keys: bfloat16 [4, 512, 1024], P('section', 'cp', 'tp'), may hold values from -4 to 4
- values: bfloat16 [4, 512, 1024], P('section', 'cp', 'tp'), may hold values from -6 to 6
- grads: bfloat16 [4, 512, 8192], P('section', 'cp', 'tp'), may hold values from -6 to 6
- docs: int32 [4, 512], P('section'), may hold values from 0 to 7, never falling along the last dimension, each value on 1 to 256 neighbouring positions
- order: int32 [4, 512], P('section'), may hold values from 0 to 511, each once within a row
Outputs:
- outputs: bfloat16 [4, 512, 8192], P('section', 'cp', 'tp')
- grad_query: bfloat16 [4, 512, 8192], P('section', 'cp', 'tp')
- grad_keys: bfloat16 [4, 512, 1024], P('section', 'cp', 'tp')
- grad_values: bfloat16 [4, 512, 1024], P('section', 'cp', 'tp')
Inputs may be any that keep to these rules, and one draw needn't show every extreme that they name: `docs`: along positions of one section the document numbers never fall; each document holds 1 to 256 tokens. `order`: each section's row holds every position once.
All inputs are finite; a program needn't handle non-finite values.
Results may differ from a plain program's by a relative error of at most 0.0061.
Values may be sent and summed in bfloat16 or wider, within the bound.
A program may use at most 64 MiB of HBM per device.

v0:
```python
import jax
import jax.numpy as jnp
from jax import lax
from jax.sharding import PartitionSpec as P

HEAD = 128


def passed_along(block, axis, distance):
    devices = range(lax.axis_size(axis))
    route = [((i - distance) % len(devices), i) for i in devices]
    return lax.ppermute(block, axis, route)


def split_heads(block, kv_count):
    tokens = block.shape[0]
    group = block.shape[1] // (kv_count * HEAD)
    return (
        block.reshape(tokens, kv_count, group, HEAD)
        .transpose(1, 2, 0, 3)
        .reshape(kv_count, group * tokens, HEAD)
    )


def join_heads(rows, tokens):
    kv_count = rows.shape[0]
    group = rows.shape[1] // tokens
    return (
        rows.reshape(kv_count, group, tokens, HEAD)
        .transpose(2, 0, 1, 3)
        .reshape(tokens, kv_count * group * HEAD)
    )


def forward_part(flat_q, key, value, allowed):
    scale = HEAD ** (-0.5)
    rows_q = allowed.shape[0]
    scores = (
        lax.dot_general(flat_q, key, (((1,), (1,)), ((), ())), preferred_element_type=jnp.float32)
        * scale
    )
    scores = scores.reshape(-1, rows_q, key.shape[0])
    scores = jnp.where(allowed[None], scores, -jnp.inf)
    peak = jnp.max(scores, axis=2, keepdims=True)
    expd = jnp.exp(scores - peak)
    probs = (expd / jnp.sum(expd, axis=2, keepdims=True)).astype(jnp.bfloat16)
    probs = probs.reshape(flat_q.shape[0], key.shape[0])
    attended = jnp.dot(probs, value, preferred_element_type=jnp.float32)
    return (probs, attended)


def backward_part(probs, attended, flat_g, key, value):
    scale = HEAD ** (-0.5)
    delta = jnp.sum(flat_g.astype(jnp.float32) * attended, axis=1, keepdims=True)
    dprob = lax.dot_general(
        flat_g, value, (((1,), (1,)), ((), ())), preferred_element_type=jnp.float32
    )
    dscore = (probs.astype(jnp.float32) * (dprob - delta)).astype(jnp.bfloat16)
    dquery = jnp.dot(dscore, key, preferred_element_type=jnp.float32) * scale
    return (dscore, dquery)


def key_terms(probs, dscore, flat_q, flat_g):
    scale = HEAD ** (-0.5)
    dkey = (
        lax.dot_general(
            dscore, flat_q, (((0,), (0,)), ((), ())), preferred_element_type=jnp.float32
        )
        * scale
    )
    dvalue = lax.dot_general(
        probs, flat_g, (((0,), (0,)), ((), ())), preferred_element_type=jnp.float32
    )
    return (dkey, dvalue)


def stack_terms(dkeys, dvalues):
    count = dkeys.shape[1]
    return jnp.concatenate(
        [
            dkeys.transpose(1, 0, 2).reshape(count, -1),
            dvalues.transpose(1, 0, 2).reshape(count, -1),
        ],
        axis=1,
    )


def on_device(acts, keys, values, grads, docs, order):
    tok = acts.shape[1]
    kv_count = keys.shape[2] // HEAD
    width = kv_count * HEAD
    query = passed_along(acts, "section", 1)[0]
    cotan = passed_along(grads, "section", -1)[0]
    key_all, value_all = (
        lax.all_gather(keys[0], "cp", axis=0, tiled=True),
        lax.all_gather(values[0], "cp", axis=0, tiled=True),
    )
    positions = order[0]
    doc_all = jnp.take(docs[0], positions)
    first = lax.axis_index("cp") * tok
    my_pos = lax.dynamic_slice_in_dim(positions, first, tok)
    my_doc = lax.dynamic_slice_in_dim(doc_all, first, tok)
    allowed = (my_doc[:, None] == doc_all[None, :]) & (positions[None, :] <= my_pos[:, None])
    q_rows = split_heads(query, kv_count)
    k_heads = key_all.reshape(-1, kv_count, HEAD).transpose(1, 0, 2)
    v_heads = value_all.reshape(-1, kv_count, HEAD).transpose(1, 0, 2)
    probs, attended = lax.map(
        lambda parts: forward_part(parts[0], parts[1], parts[2], allowed),
        (q_rows, k_heads, v_heads),
    )
    outputs = (query.astype(jnp.float32) + join_heads(attended, tok)).astype(jnp.bfloat16)
    g_rows = split_heads(cotan, kv_count)
    dscores, dqueries = lax.map(
        lambda parts: backward_part(parts[0], parts[1], parts[2], parts[3], parts[4]),
        (probs, attended, g_rows, k_heads, v_heads),
    )
    grad_query = (cotan.astype(jnp.float32) + join_heads(dqueries, tok)).astype(jnp.bfloat16)
    dkeys, dvalues = jax.vmap(key_terms)(probs, dscores, q_rows, g_rows)
    summed = lax.psum_scatter(stack_terms(dkeys, dvalues), "cp", scatter_dimension=0, tiled=True)
    grad_keys = summed[:, :width].astype(jnp.bfloat16)
    grad_values = summed[:, width:].astype(jnp.bfloat16)
    return (outputs[None], grad_query[None], grad_keys[None], grad_values[None])


def solution(mesh):
    placed = (
        P("section", "cp", "tp"),
        P("section", "cp", "tp"),
        P("section", "cp", "tp"),
        P("section", "cp", "tp"),
        P("section", None),
        P("section", None),
    )
    return jax.shard_map(
        on_device,
        mesh=mesh,
        in_specs=placed,
        out_specs=(
            P("section", "cp", "tp"),
            P("section", "cp", "tp"),
            P("section", "cp", "tp"),
            P("section", "cp", "tp"),
        ),
        check_vma=False,
    )
```

profile of v0, /device:TPU:0, one launch (start us, length us, event | category | flops | bytes accessed | tf_op | source)
XLA Modules:
  0.0 176.0 jit_solution(15219660777080566842)
XLA Ops:
  7.2 3.0 %collective-permute-start = (bf16[1,128,4096]{2,1,0:T(8,128)(2,1)}, bf16[1,128,4096]{2,1,0:T(8,128)(2,1)S(1)}, u32[]{:S(2)}, u32[]{:S(2)}) collective-permute-start(bf16[1,128,4096]{2,1,0:T(8,128)(2,1)} %param.10), channel_id=1, source_target_pairs={{24,0},{0,8},{8,16},{16,24},{25,1},{1,9},{9,17},{17,25},{26,2},{2,... | collective-permute-start | bytes 3145736 | tf_op jit(solution)/shard_map/ppermute | solution.py:12
  10.3 1.0 collective-permute-start.1
  11.3 1.0 copy.22
  12.3 15.2 %all-gather = bf16[1,512,512]{1,2,0:T(8,128)(2,1)S(1)} all-gather(bf16[1,128,512]{1,2,0:T(8,128)(2,1)S(1)} %copy.22), channel_id=2, replica_groups=mesh['section'=4,'cp'=4,'tp'=2] {'cp'}, dimensions={1}, use_global_device_ids=true | all-gather | bytes 655360 | tf_op jit(solution)/shard_map/all_gather | solution.py:95
  27.5 1.0 copy.25
  28.5 1.0 copy.23
  29.5 14.3 %all-gather.1 = bf16[1,512,512]{1,2,0:T(8,128)(2,1)S(1)} all-gather(bf16[1,128,512]{1,2,0:T(8,128)(2,1)S(1)} %copy.23), channel_id=3, replica_groups=mesh['section'=4,'cp'=4,'tp'=2] {'cp'}, dimensions={1}, use_global_device_ids=true | all-gather | bytes 655360 | tf_op jit(solution)/shard_map/all_gather | solution.py:96
  43.8 1.0 copy.26
  44.9 3.5 %gather_fusion = s32[512]{0:T(512)S(1)} fusion(s32[512]{0:T(512)S(1)} %bitcast.141, s32[1024]{0:T(1024)S(1)} %pad_clamp_fusion), kind=kCustom, calls=%fused_computation | custom fusion | bytes 6144 | tf_op jit(solution)/shard_map/jit(_take)/gather | solution.py:99
  48.8 0.7 copy-done.4
  49.5 1.2 copy.21
  51.2 1.5 broadcast.70.clone
  52.7 23.3 %while.26 = (s32[]{:T(128)}, bf16[4,1024,512]{1,2,0:T(8,128)(2,1)}, f32[4,1024,128]{2,1,0:T(8,128)}, bf16[4,1024,128]{1,2,0:T(8,128)(2,1)S(1)}, bf16[4,512,128]{...) while((s32[]{:T(128)}, bf16[4,1024,512]{1,2,0:T(8,128)(2,1)}, ...), condition=%wide.region_3.4_spmd.clone, body=%wide.region_0.3_spmd.clone.sunk | while | flops 274397184 | bytes 11701869 | solution.py:107
  53.2 1.5 fusion.43
  55.0 2.3 %fusion.45 = f32[4,1024,128]{2,1,0:T(8,128)} fusion(f32[4,1024,128]{2,1,0:T(8,128)} %get-tuple-element.324, s32[]{:T(128)} %get-tuple-element.322, bf16[4,512,128]{2,1,0:T(8,128)(2,1)} %get-tuple-element.338, f32[1024,512]{0,1:T(8,128)S(1)} %get-tuple-element.309, f32[1024]{0:T(1024)S(1)} %fusion.44, f32[1024]{0:T(1024)S(1)} %get-tuple-element.310), kind=kOutput, calls=%fused_computation.24.clone.1 | convolution fusion | flops 135790592 | bytes 2761728 | tf_op jit(solution)/shard_map/while/body/eval_jaxpr/dot_general | solution.py:48
  57.2 1.3 bitcast_dynamic-update-slice_fusion.5
  59.0 1.4 fusion.43
  60.8 2.3 %fusion.45 = f32[4,1024,128]{2,1,0:T(8,128)} fusion(f32[4,1024,128]{2,1,0:T(8,128)} %get-tuple-element.324, s32[]{:T(128)} %get-tuple-element.322, bf16[4,512,128]{2,1,0:T(8,128)(2,1)} %get-tuple-element.338, f32[1024,512]{0,1:T(8,128)S(1)} %get-tuple-element.309, f32[1024]{0:T(1024)S(1)} %fusion.44, f32[1024]{0:T(1024)S(1)} %get-tuple-element.310), kind=kOutput, calls=%fused_computation.24.clone.1 | convolution fusion | flops 135790592 | bytes 2761728 | tf_op jit(solution)/shard_map/while/body/eval_jaxpr/dot_general | solution.py:48
  63.0 1.3 bitcast_dynamic-update-slice_fusion.5
  64.8 1.5 fusion.43
  66.6 2.2 %fusion.45 = f32[4,1024,128]{2,1,0:T(8,128)} fusion(f32[4,1024,128]{2,1,0:T(8,128)} %get-tuple-element.324, s32[]{:T(128)} %get-tuple-element.322, bf16[4,512,128]{2,1,0:T(8,128)(2,1)} %get-tuple-element.338, f32[1024,512]{0,1:T(8,128)S(1)} %get-tuple-element.309, f32[1024]{0:T(1024)S(1)} %fusion.44, f32[1024]{0:T(1024)S(1)} %get-tuple-element.310), kind=kOutput, calls=%fused_computation.24.clone.1 | convolution fusion | flops 135790592 | bytes 2761728 | tf_op jit(solution)/shard_map/while/body/eval_jaxpr/dot_general | solution.py:48
  68.9 1.3 bitcast_dynamic-update-slice_fusion.5
  70.6 1.5 fusion.43
  72.4 2.2 %fusion.45 = f32[4,1024,128]{2,1,0:T(8,128)} fusion(f32[4,1024,128]{2,1,0:T(8,128)} %get-tuple-element.324, s32[]{:T(128)} %get-tuple-element.322, bf16[4,512,128]{2,1,0:T(8,128)(2,1)} %get-tuple-element.338, f32[1024,512]{0,1:T(8,128)S(1)} %get-tuple-element.309, f32[1024]{0:T(1024)S(1)} %fusion.44, f32[1024]{0:T(1024)S(1)} %get-tuple-element.310), kind=kOutput, calls=%fused_computation.24.clone.1 | convolution fusion | flops 135790592 | bytes 2761728 | tf_op jit(solution)/shard_map/while/body/eval_jaxpr/dot_general | solution.py:48
  74.7 1.3 bitcast_dynamic-update-slice_fusion.5
  76.0 1.0 copy-done.6
  77.0 1.4 copy.44
  78.5 1.2 copy.28
  80.2 4.8 %fusion.24 = f32[4,512,128]{1,2,0:T(8,128)} fusion(bf16[4,1024,512]{1,2,0:T(8,128)(2,1)} %get-tuple-element.347, bf16[4,1024,128]{1,2,0:T(8,128)(2,1)S(1)} %reshape.120), kind=kOutput, calls=%fused_computation.51 | convolution fusion | flops 536870912 | bytes 6291456 | tf_op jit(solution)/shard_map/vmap()/dot_general | solution.py:71
  85.0 1.5 broadcast.70
  86.4 31.5 %while.25 = (s32[]{:T(128)}, bf16[4,1024,512]{2,1,0:T(8,128)(2,1)}, f32[4,1024,128]{2,1,0:T(8,128)}, bf16[4,1024,512]{1,2,0:T(8,128)(2,1)}, bf16[4,1024,128]{1,2...) while((s32[]{:T(128)}, bf16[4,1024,512]{2,1,0:T(8,128)(2,1)}, ...), condition=%wide.region_6.7_spmd, body=%wide.region_4.6_spmd.sunk | while | flops 271055872 | bytes 11283049 | solution.py:113
  86.6 1.3 fusion.40
  87.9 1.3 constant_dynamic-slice_fusion.6
  89.2 0.5 copy.53
  89.8 2.4 %bitcast_dynamic-update-slice_fusion.4 = (bf16[4,1024,512]{2,1,0:T(8,128)(2,1)}, bf16[1024,512]{1,0:T(8,128)(2,1)S(1)}) fusion(bf16[4,1024,512]{2,1,0:T(8,128)(2,1)} %get-tuple-element.354, s32[]{:T(128)} %get-tuple-element.353, f32[1024]{0:T(1024)S(1)} %fusion.40, bf16[4,512,128]{2,1,0:T(8,128)(2,1)} %get-tuple-element.367, ...), kind=kOutput, calls=%fused_computation.7.clone.1 | convolution fusion | flops 136314880 | bytes 3544576 | tf_op jit(solution)/shard_map/while/body/eval_jaxpr/dot_general | solution.py:55
  92.1 2.2 %fusion.41 = f32[4,1024,128]{2,1,0:T(8,128)} fusion(f32[4,1024,128]{2,1,0:T(8,128)} %get-tuple-element.355, s32[]{:T(128)} %get-tuple-element.353, bf16[1024,512]{1,0:T(8,128)(2,1)S(1)} %get-tuple-element.298, bf16[4,512,128]{2,1,0:T(8,128)(2,1)} %get-tuple-element.369), kind=kOutput, calls=%fused_computation.6.clone.1 | convolution fusion | flops 134348800 | bytes 1704960 | tf_op jit(solution)/shard_map/while/body/eval_jaxpr/dot_general | solution.py:59
  94.5 1.3 fusion.40
  95.8 1.3 constant_dynamic-slice_fusion.6
  97.1 0.5 copy.53
  97.6 2.4 %bitcast_dynamic-update-slice_fusion.4 = (bf16[4,1024,512]{2,1,0:T(8,128)(2,1)}, bf16[1024,512]{1,0:T(8,128)(2,1)S(1)}) fusion(bf16[4,1024,512]{2,1,0:T(8,128)(2,1)} %get-tuple-element.354, s32[]{:T(128)} %get-tuple-element.353, f32[1024]{0:T(1024)S(1)} %fusion.40, bf16[4,512,128]{2,1,0:T(8,128)(2,1)} %get-tuple-element.367, ...), kind=kOutput, calls=%fused_computation.7.clone.1 | convolution fusion | flops 136314880 | bytes 3544576 | tf_op jit(solution)/shard_map/while/body/eval_jaxpr/dot_general | solution.py:55
  100.1 2.1 %fusion.41 = f32[4,1024,128]{2,1,0:T(8,128)} fusion(f32[4,1024,128]{2,1,0:T(8,128)} %get-tuple-element.355, s32[]{:T(128)} %get-tuple-element.353, bf16[1024,512]{1,0:T(8,128)(2,1)S(1)} %get-tuple-element.298, bf16[4,512,128]{2,1,0:T(8,128)(2,1)} %get-tuple-element.369), kind=kOutput, calls=%fused_computation.6.clone.1 | convolution fusion | flops 134348800 | bytes 1704960 | tf_op jit(solution)/shard_map/while/body/eval_jaxpr/dot_general | solution.py:59
  102.4 1.3 fusion.40
  103.7 1.3 constant_dynamic-slice_fusion.6
  105.0 0.5 copy.53
  105.5 2.4 %bitcast_dynamic-update-slice_fusion.4 = (bf16[4,1024,512]{2,1,0:T(8,128)(2,1)}, bf16[1024,512]{1,0:T(8,128)(2,1)S(1)}) fusion(bf16[4,1024,512]{2,1,0:T(8,128)(2,1)} %get-tuple-element.354, s32[]{:T(128)} %get-tuple-element.353, f32[1024]{0:T(1024)S(1)} %fusion.40, bf16[4,512,128]{2,1,0:T(8,128)(2,1)} %get-tuple-element.367, ...), kind=kOutput, calls=%fused_computation.7.clone.1 | convolution fusion | flops 136314880 | bytes 3544576 | tf_op jit(solution)/shard_map/while/body/eval_jaxpr/dot_general | solution.py:55
  107.9 2.1 %fusion.41 = f32[4,1024,128]{2,1,0:T(8,128)} fusion(f32[4,1024,128]{2,1,0:T(8,128)} %get-tuple-element.355, s32[]{:T(128)} %get-tuple-element.353, bf16[1024,512]{1,0:T(8,128)(2,1)S(1)} %get-tuple-element.298, bf16[4,512,128]{2,1,0:T(8,128)(2,1)} %get-tuple-element.369), kind=kOutput, calls=%fused_computation.6.clone.1 | convolution fusion | flops 134348800 | bytes 1704960 | tf_op jit(solution)/shard_map/while/body/eval_jaxpr/dot_general | solution.py:59
  110.3 1.3 fusion.40
  111.5 1.3 constant_dynamic-slice_fusion.6
  113.4 2.4 %bitcast_dynamic-update-slice_fusion.4 = (bf16[4,1024,512]{2,1,0:T(8,128)(2,1)}, bf16[1024,512]{1,0:T(8,128)(2,1)S(1)}) fusion(bf16[4,1024,512]{2,1,0:T(8,128)(2,1)} %get-tuple-element.354, s32[]{:T(128)} %get-tuple-element.353, f32[1024]{0:T(1024)S(1)} %fusion.40, bf16[4,512,128]{2,1,0:T(8,128)(2,1)} %get-tuple-element.367, ...), kind=kOutput, calls=%fused_computation.7.clone.1 | convolution fusion | flops 136314880 | bytes 3544576 | tf_op jit(solution)/shard_map/while/body/eval_jaxpr/dot_general | solution.py:55
  115.8 2.1 %fusion.41 = f32[4,1024,128]{2,1,0:T(8,128)} fusion(f32[4,1024,128]{2,1,0:T(8,128)} %get-tuple-element.355, s32[]{:T(128)} %get-tuple-element.353, bf16[1024,512]{1,0:T(8,128)(2,1)S(1)} %get-tuple-element.298, bf16[4,512,128]{2,1,0:T(8,128)(2,1)} %get-tuple-element.369), kind=kOutput, calls=%fused_computation.6.clone.1 | convolution fusion | flops 134348800 | bytes 1704960 | tf_op jit(solution)/shard_map/while/body/eval_jaxpr/dot_general | solution.py:59
  117.9 3.2 %convolution_multiply_fusion.1 = f32[4,512,128]{1,2,0:T(8,128)S(1)} fusion(bf16[4,1024,128]{1,2,0:T(8,128)(2,1)} %copy-done.3, bf16[4,1024,512]{2,1,0:T(8,128)(2,1)} %get-tuple-element.88), kind=kOutput, calls=%fused_computation.40 | convolution fusion | flops 537133056 | bytes 6291456 | tf_op jit(solution)/shard_map/vmap()/dot_general | solution.py:66
  121.5 0.9 copy-done.8
  122.7 1.5 pad_maximum_fusion
  124.3 1.6 copy-done.1
  125.9 2.5 %copy.48 = f32[4,8,128,128]{3,1,0,2:T(8,128)} copy(f32[4,8,128,128]{3,2,1,0:T(8,128)S(1)} %bitcast.143) | data formatting | bytes 4194304 | tf_op jit(solution)/shard_map/reshape | solution.py:29
  128.4 1.9 %reshape.122 = f32[1,128,4096]{2,1,0:T(8,128)S(1)} reshape(f32[128,4,8,128]{3,2,1,0:T(8,128)} %bitcast.144) | data formatting | bytes 4194304 | tf_op jit(solution)/shard_map/reshape | solution.py:31
  130.3 4.1 %copy.49 = f32[4,8,128,128]{3,1,0,2:T(8,128)} copy(f32[4,8,128,128]{3,2,1,0:T(8,128)} %bitcast.19) | data formatting | bytes 4194304 | tf_op jit(solution)/shard_map/reshape | solution.py:29
  134.4 2.9 %reshape.119 = f32[1,128,4096]{2,1,0:T(8,128)} reshape(f32[128,4,8,128]{3,2,1,0:T(8,128)} %bitcast.145) | data formatting | bytes 4194304 | tf_op jit(solution)/shard_map/reshape | solution.py:31
  137.3 1.2 add_convert_fusion
  138.5 0.8 copy-done.2
  139.5 1.2 add_convert_fusion.1
  140.7 26.7 %reduce-scatter.2.cloned.1.call-done = f32[128,1024]{1,0:T(8,128)} async-done(((f32[512,1024]{1,0:T(8,128)}), f32[128,1024]{1,0:T(8,128)}) %reduce-scatter.2.cloned.1.call-update) | async-done | bytes 524304 | tf_op jit(solution)/shard_map/reduce_scatter | solution.py:119
  167.4 1.1 convert.5
  168.5 0.7 slice_bitcast_fusion
  (53 shorter events, 6.8 us)
Async XLA Ops:
  7.2 37.7 %copy-start = (s32[1,512]{1,0:T(1,128)S(1)}, s32[1,512]{1,0:T(1,128)}, u32[]{:S(2)}) copy-start(s32[1,512]{1,0:T(1,128)} %param.14) | copy-start | bytes 6148
  7.2 37.7 %copy-start.9 = (s32[1,512]{1,0:T(1,128)S(1)}, s32[1,512]{1,0:T(1,128)}, u32[]{:S(2)}) copy-start(s32[1,512]{1,0:T(1,128)} %param.15) | copy-start | bytes 6148
  7.2 160.2 %reduce-scatter.2.cloned.1.call-start = ((), (), s32[]{:S(2)}) async-start(), calls=%async_computation.1 | async-start | bytes 2621440 | tf_op jit(solution)/shard_map/reduce_scatter | solution.py:119
  7.2 41.3 %collective-permute-start = (bf16[1,128,4096]{2,1,0:T(8,128)(2,1)}, bf16[1,128,4096]{2,1,0:T(8,128)(2,1)S(1)}, u32[]{:S(2)}, u32[]{:S(2)}) collective-permute-start(bf16[1,128,4096]{2,1,0:T(8,128)(2,1)} %param.10), channel_id=1, source_target_pairs={{24,0},{0,8},{8,16},{16,24},{25,1},{1,9},{9,17},{17,25},{26,2},{2,... | collective-permute-start | bytes 3145736 | tf_op jit(solution)/shard_map/ppermute | solution.py:12
  10.3 65.8 %collective-permute-start.1 = (bf16[1,128,4096]{2,1,0:T(8,128)(2,1)}, bf16[1,128,4096]{2,1,0:T(8,128)(2,1)S(1)}, u32[]{:S(2)}, u32[]{:S(2)}) collective-permute-start(bf16[1,128,4096]{2,1,0:T(8,128)(2,1)} %param.13), channel_id=1, source_target_pairs={{8,0},{16,8},{24,16},{0,24},{9,1},{17,9},{25,17},{1,25},{10,2},{18... | collective-permute-start | bytes 3145736 | tf_op jit(solution)/shard_map/ppermute | solution.py:12
  48.5 1.0 copy-start.4
  76.0 3.7 %copy-start.3 = (bf16[4,1024,128]{1,2,0:T(8,128)(2,1)}, bf16[4,1024,128]{1,2,0:T(8,128)(2,1)S(1)}, u32[]{:S(2)}) copy-start(bf16[4,1024,128]{1,2,0:T(8,128)(2,1)S(1)} %get-tuple-element.374) | copy-start | bytes 3145732
  76.0 1.0 copy-start.6
  121.2 1.2 copy-start.8
  124.3 1.6 copy-start.1
  134.4 2.9 %copy-start.7 = (bf16[1,128,4096]{2,1,0:T(8,128)(2,1)S(1)}, bf16[1,128,4096]{2,1,0:T(8,128)(2,1)}, u32[]{:S(2)}) copy-start(bf16[1,128,4096]{2,1,0:T(8,128)(2,1)} %copy-done.6) | copy-start | bytes 3145732
  137.3 2.0 %copy-start.2 = (f32[1,128,4096]{2,1,0:T(8,128)S(1)}, f32[1,128,4096]{2,1,0:T(8,128)}, u32[]{:S(2)}) copy-start(f32[1,128,4096]{2,1,0:T(8,128)} %reshape.119) | copy-start | bytes 6291460
  137.3 2.2 %copy-start.5 = (bf16[1,128,4096]{2,1,0:T(8,128)(2,1)S(1)}, bf16[1,128,4096]{2,1,0:T(8,128)(2,1)}, u32[]{:S(2)}) copy-start(bf16[1,128,4096]{2,1,0:T(8,128)(2,1)} %copy-done.4) | copy-start | bytes 3145732
Sparse Core Ops, SparseCore 0:
  124.4 42.9 reduce-scatter.1
where the time goes:
time: 177 us; the launch traced here: 176 us
  local copies, waits for them, and re-layouts  42.9 us (24%)
  matrix products  41 us (23%)
  blocking collectives  29.5 us (17%)
  waiting for transfers between devices  26.7 us (15%)
  other arithmetic  17.5 us (10%)
  between operations  14.2 us (8%)
  starting transfers between devices  4.08 us (2%)
    reduce_scatter x1, waiting for transfers between devices, on_device(): lax.psum_scatter(stack_terms(dkeys, dvalues), 'cp', scatter_dimension=0,...  26.7 us
    all_gather x1, blocking collectives, on_device(): lax.all_gather(keys[0], 'cp', axis=0, tiled=True)  15.2 us
    all_gather x1, blocking collectives, on_device(): lax.all_gather(values[0], 'cp', axis=0, tiled=True)  14.3 us
    unnamed x26, local copies, waits for them, and re-layouts  11 us
    dot_general x4, matrix products, backward_part(): lax.dot_general(flat_g, value, (((1,), (1,)), ((), ())), preferred_elemen...  9.64 us
    dot_general x4, matrix products, forward_part(): attended = jnp.dot(probs, value, preferred_element_type=jnp.float32)  9 us
    dot_general x4, matrix products, backward_part(): dquery = jnp.dot(dscore, key, preferred_element_type=jnp.float32) * scale  8.56 us
    dynamic_slice x8, local copies, waits for them, and re-layouts, on_device(): lax.map(lambda parts: backward_part(parts[0], parts[1], parts[2], parts[3...  7.37 us
  transfers between devices with their start and end apart: 3, of which 1 were waited for; matrix products, arithmetic and copies ran while one was open for 27% of the time, Pallas kernels for 0%

commit v1 on v0

v1 whole, which is shorter than its diff:
```python
import functools

import jax
import jax.numpy as jnp
from jax import lax
from jax.experimental import pallas as pl
from jax.experimental.pallas import tpu as pltpu
from jax.sharding import PartitionSpec as P

HEAD = 128
DOCS = 8


def passed_along(block, axis, distance):
    devices = range(lax.axis_size(axis))
    route = [((i - distance) % len(devices), i) for i in devices]
    return lax.ppermute(block, axis, route)


def times(a, b, dims):
    return lax.dot_general(a, b, (dims, ((), ())), preferred_element_type=jnp.float32)


def attention_kernel(group, pack, aliased, *refs):
    q_ref, g_ref, k_ref, v_ref, bias_ref = refs[:5]
    out_ref, gq_ref, terms_ref, dk_ref, dv_ref = refs[7:] if aliased else refs[5:]
    scale = HEAD ** (-0.5)
    rows = q_ref.shape[1]
    k, v = k_ref[...], v_ref[...]
    k_t, v_t = k.T, v.T
    for first in range(0, group, pack):
        cols = [slice((first + j) * HEAD, (first + j + 1) * HEAD) for j in range(pack)]
        q = jnp.concatenate([q_ref[0, :, c] for c in cols], axis=0)
        g = jnp.concatenate([g_ref[0, :, c] for c in cols], axis=0)
        scores = times(k, q, ((1,), (1,))) * scale + bias_ref[...]
        expd = jnp.exp(scores - jnp.max(scores, axis=0, keepdims=True))
        probs = (expd * (1.0 / jnp.sum(expd, axis=0, keepdims=True))).astype(jnp.bfloat16)
        attended = times(v_t, probs, ((1,), (0,))).T
        dprob = times(v, g, ((1,), (1,)))
        wide = probs.astype(jnp.float32)
        delta = jnp.sum(wide * dprob, axis=0, keepdims=True)
        dscore = (wide * (dprob - delta)).astype(jnp.bfloat16)
        dquery = times(k_t, dscore, ((1,), (0,))).T
        out = (q.astype(jnp.float32) + attended).astype(jnp.bfloat16)
        gq = (g.astype(jnp.float32) + dquery * scale).astype(jnp.bfloat16)
        for j, c in enumerate(cols):
            out_ref[0, :, c] = out[j * rows : (j + 1) * rows]
            gq_ref[0, :, c] = gq[j * rows : (j + 1) * rows]
        dk = times(dscore, q, ((1,), (0,)))
        dv = times(probs, g, ((1,), (0,)))
        if first == 0:
            dk_ref[...] = dk
            dv_ref[...] = dv
        else:
            dk_ref[...] += dk
            dv_ref[...] += dv
    terms_ref[:, :HEAD] = (dk_ref[...] * scale).astype(jnp.bfloat16)
    terms_ref[:, HEAD:] = dv_ref[...].astype(jnp.bfloat16)


def attention(query, cotan, key_all, value_all, bias, head0, heads, whole_shape, partial):
    tok = query.shape[1]
    count = key_all.shape[0]
    width = query.shape[2] // heads
    group = width // HEAD
    pack = bias.shape[1] // tok
    aliased = partial is not None
    any_spec = pl.BlockSpec(memory_space=pl.ANY)
    chunk = pl.BlockSpec((1, tok, width), lambda h: (0, 0, h))
    kv = pl.BlockSpec((count, HEAD), lambda h: (0, head0 + h))
    result = pl.BlockSpec((1, tok, width), lambda h: (0, 0, head0 + h))
    pairs = group * heads * tok * count
    return pl.pallas_call(
        functools.partial(attention_kernel, group, pack, aliased),
        grid=(heads,),
        out_shape=(
            jax.ShapeDtypeStruct(whole_shape, jnp.bfloat16),
            jax.ShapeDtypeStruct(whole_shape, jnp.bfloat16),
            jax.ShapeDtypeStruct((count, heads * 2 * HEAD), jnp.bfloat16),
        ),
        in_specs=[chunk, chunk, kv, kv, pl.BlockSpec(bias.shape, lambda h: (0, 0))]
        + [any_spec, any_spec] * aliased,
        out_specs=(result, result, pl.BlockSpec((count, 2 * HEAD), lambda h: (0, h))),
        scratch_shapes=[pltpu.VMEM((count, HEAD), jnp.float32)] * 2,
        input_output_aliases={5: 0, 6: 1} if aliased else {},
        compiler_params=pltpu.CompilerParams(vmem_limit_bytes=48 * 1024 * 1024),
        cost_estimate=pl.CostEstimate(
            flops=12 * HEAD * pairs,
            bytes_accessed=8 * tok * width * heads + 8 * count * heads * HEAD,
            transcendentals=pairs,
        ),
    )(query, cotan, key_all, value_all, bias, *(partial if aliased else ()))


def summed_over(terms, axis, tok):
    devices = lax.axis_size(axis)
    me = lax.axis_index(axis)
    total = lax.dynamic_slice_in_dim(terms, me * tok, tok).astype(jnp.float32)
    for step in range(1, devices):
        there = lax.rem(me + step, devices)
        block = lax.dynamic_slice_in_dim(terms, there * tok, tok)
        total = total + passed_along(block, axis, step).astype(jnp.float32)
    return total


def on_device(acts, keys, values, grads, docs, order):
    tok = acts.shape[1]
    kv_count = keys.shape[2] // HEAD
    width = acts.shape[2] // kv_count
    group = width // HEAD
    pack = 2 if group % 2 == 0 else 1
    chunks = 2 if kv_count % 2 == 0 else 1
    heads = kv_count // chunks
    moved = []
    for c in range(chunks):
        cols = slice(c * heads * width, (c + 1) * heads * width)
        moved.append(
            (
                passed_along(acts[:, :, cols], "section", 1),
                passed_along(grads[:, :, cols], "section", -1),
            )
        )
    key_all = lax.all_gather(keys[0], "cp", axis=0, tiled=True)
    value_all = lax.all_gather(values[0], "cp", axis=0, tiled=True)

    positions = order[0]
    starts = jnp.sum(docs[0][None, :] < jnp.arange(1, DOCS)[:, None], axis=1)
    first = lax.axis_index("cp") * tok
    mine = lax.dynamic_slice_in_dim(positions, first, tok)
    low = jnp.max(jnp.where(starts[:, None] <= mine[None, :], starts[:, None], 0), axis=0)
    allowed = (positions[:, None] <= mine[None, :]) & (positions[:, None] >= low[None, :])
    bias = jnp.tile(jnp.where(allowed, 0.0, -1e30).astype(jnp.float32), (1, pack))

    partial, parts = None, []
    for c, (query, cotan) in enumerate(moved):
        out, gq, terms = attention(
            query, cotan, key_all, value_all, bias, c * heads, heads, acts.shape, partial
        )
        partial = (out, gq)
        parts.append(summed_over(terms, "cp", tok).astype(jnp.bfloat16))
    total = jnp.concatenate(parts, axis=1).reshape(tok, kv_count, 2, HEAD)
    grad_keys = total[:, :, 0].reshape(tok, kv_count * HEAD)
    grad_values = total[:, :, 1].reshape(tok, kv_count * HEAD)
    return (partial[0], partial[1], grad_keys[None], grad_values[None])


def solution(mesh):
    placed = (
        P("section", "cp", "tp"),
        P("section", "cp", "tp"),
        P("section", "cp", "tp"),
        P("section", "cp", "tp"),
        P("section", None),
        P("section", None),
    )
    return jax.shard_map(
        on_device,
        mesh=mesh,
        in_specs=placed,
        out_specs=(
            P("section", "cp", "tp"),
            P("section", "cp", "tp"),
            P("section", "cp", "tp"),
            P("section", "cp", "tp"),
        ),
        check_vma=False,
    )
```

time: 177 us -> 82.3 us (0.46)
  matrix products: 41 us -> 0 us
  local copies, waits for them, and re-layouts: 42.9 us -> 9.04 us
  waiting for transfers between devices: 26.7 us -> 5.05 us
  Pallas kernels: 0 us -> 19 us
  other arithmetic: 17.5 us -> 0.59 us
  between operations: 14.2 us -> 0.75 us
  starting transfers between devices: 4.08 us -> 16.1 us
  blocking collectives: 29.5 us -> 31.6 us
    dot_general x18 -> x0, matrix products: 41 us -> none  [the longest x4 9.64 us: backward_part(): lax.dot_general(flat_g, value, (((1,), (1,)), ((), ())), preferred_elemen...]
    reduce_scatter x1 -> x0, waiting for transfers between devices: 26.7 us -> none  [on_device(): lax.psum_scatter(stack_terms(dkeys, dvalues), 'cp', scatter_dimension=0,...]
    pallas_call x0 -> x2, Pallas kernels: none -> 19 us  [attention(): pl.pallas_call(functools.partial(attention_kernel, group, pack, aliased),...]
    reshape x8 -> x1, local copies, waits for them, and re-layouts: 13.1 us -> 0.17 us  [on_device(): total = jnp.concatenate(parts, axis=1).reshape(tok, kv_count, 2, HEAD)]
    ppermute x2 -> x10, starting transfers between devices: 4.04 us -> 16.1 us  [passed_along(): return lax.ppermute(block, axis, route)]
    dynamic_slice x17 -> x2, local copies, waits for them, and re-layouts: 8.2 us -> 0.05 us  [summed_over(): block = lax.dynamic_slice_in_dim(terms, there * tok, tok)]
    reduce_sum x8 -> x1, other arithmetic: 6.39 us -> 0.18 us  [on_device(): starts = jnp.sum(docs[0][None, :] < jnp.arange(1, DOCS)[:, None], axis=1)]
    unnamed x26 -> x15, local copies, waits for them, and re-layouts: 11 us -> 4.86 us
  transfers between devices with their start and end apart: 3 -> 10, of which waited for: 1 -> 2; matrix products, arithmetic and copies ran while one was open for 27% -> 2% of each run, Pallas kernels for 0% -> 23%
where the time goes in v1:
time: 82.3 us; the launch traced here: 82.1 us
  blocking collectives  31.6 us (38%)
  Pallas kernels  19 us (23%)
  starting transfers between devices  16.1 us (20%)
  local copies, waits for them, and re-layouts  9.04 us (11%)
  waiting for transfers between devices  5.05 us (6%)
    pallas_call x2, Pallas kernels, attention(): pl.pallas_call(functools.partial(attention_kernel, group, pack, aliased),...  19 us
    ppermute x10, starting transfers between devices, passed_along(): return lax.ppermute(block, axis, route)  16.1 us
    all_gather x1, blocking collectives, on_device(): value_all = lax.all_gather(values[0], 'cp', axis=0, tiled=True)  15.9 us
    all_gather x1, blocking collectives, on_device(): key_all = lax.all_gather(keys[0], 'cp', axis=0, tiled=True)  15.7 us
    ppermute x10, waiting for transfers between devices, passed_along(): return lax.ppermute(block, axis, route)  5.05 us
    unnamed x15, local copies, waits for them, and re-layouts  4.86 us
    slice x1, local copies, waits for them, and re-layouts, on_device(): acts[:, :, cols]  2.36 us
  transfers between devices with their start and end apart: 10, of which 2 were waited for; matrix products, arithmetic and copies ran while one was open for 2% of the time, Pallas kernels for 23%

profile of v1, /device:TPU:0, one launch (start us, length us, event | category | flops | bytes accessed | tf_op | source)
XLA Modules:
  0.0 82.1 jit_solution(7652510771771697827)
XLA Ops:
  0.6 0.0 copy-start
  0.6 2.4 %fusion.2 = (bf16[1,128,2048]{2,1,0:T(8,128)(2,1)}, bf16[1,128,2048]{2,1,0:T(8,128)(2,1)}) fusion(bf16[1,128,4096]{2,1,0:T(8,128)(2,1)} %param.6), kind=kLoop, calls=%fused_computation.17 | loop fusion | bytes 2097152 | tf_op jit(solution)/shard_map/slice | solution.py:119
  3.0 3.0 %collective-permute-start.2 = (bf16[1,128,2048]{2,1,0:T(8,128)(2,1)}, bf16[1,128,2048]{2,1,0:T(8,128)(2,1)S(1)}, u32[]{:S(2)}, u32[]{:S(2)}) collective-permute-start(bf16[1,128,2048]{2,1,0:T(8,128)(2,1)} %get-tuple-element.26), channel_id=1, source_target_pairs={{24,0},{0,8},{8,16},{16,24},{25,1},{1,9},{9,17},{17,25},{26,2},{2,... | collective-permute-start | bytes 1572872 | tf_op jit(solution)/shard_map/ppermute | solution.py:17
  6.0 0.0 copy-done
  6.0 1.0 %fusion.1 = (bf16[1,128,2048]{2,1,0:T(8,128)(2,1)}, bf16[1,128,2048]{2,1,0:T(8,128)(2,1)}) fusion(bf16[1,128,4096]{2,1,0:T(8,128)(2,1)S(1)} %copy-done), kind=kLoop, calls=%fused_computation.16 | loop fusion | bytes 2097152 | tf_op jit(solution)/shard_map/slice | solution.py:120
  7.0 1.0 %collective-permute-start.3 = (bf16[1,128,2048]{2,1,0:T(8,128)(2,1)}, bf16[1,128,2048]{2,1,0:T(8,128)(2,1)S(1)}, u32[]{:S(2)}, u32[]{:S(2)}) collective-permute-start(bf16[1,128,2048]{2,1,0:T(8,128)(2,1)} %get-tuple-element.24), channel_id=1, source_target_pairs={{8,0},{16,8},{24,16},{0,24},{9,1},{17,9},{25,17},{1,25},{10,2},{18... | collective-permute-start | bytes 1572872 | tf_op jit(solution)/shard_map/ppermute | solution.py:17
  8.0 1.1 %collective-permute-start = (bf16[1,128,2048]{2,1,0:T(8,128)(2,1)}, bf16[1,128,2048]{2,1,0:T(8,128)(2,1)S(1)}, u32[]{:S(2)}, u32[]{:S(2)}) collective-permute-start(bf16[1,128,2048]{2,1,0:T(8,128)(2,1)} %get-tuple-element.27), channel_id=1, source_target_pairs={{24,0},{0,8},{8,16},{16,24},{25,1},{1,9},{9,17},{17,25},{26,2},{2,... | collective-permute-start | bytes 1572872 | tf_op jit(solution)/shard_map/ppermute | solution.py:17
  9.0 1.9 %collective-permute-start.1 = (bf16[1,128,2048]{2,1,0:T(8,128)(2,1)}, bf16[1,128,2048]{2,1,0:T(8,128)(2,1)S(1)}, u32[]{:S(2)}, u32[]{:S(2)}) collective-permute-start(bf16[1,128,2048]{2,1,0:T(8,128)(2,1)} %get-tuple-element.25), channel_id=1, source_target_pairs={{8,0},{16,8},{24,16},{0,24},{9,1},{17,9},{25,17},{1,25},{10,2},{18... | collective-permute-start | bytes 1572872 | tf_op jit(solution)/shard_map/ppermute | solution.py:17
  10.9 0.0 copy-start.3
  10.9 0.7 copy-done.3
  11.6 0.0 copy-start.4
  11.6 0.7 copy-done.4
  12.3 0.2 convert_reduce_fusion
  12.5 0.1 select_reduce_fusion
  12.5 0.0 copy-start.1
  12.5 0.1 and_select_fusion
  12.7 0.8 copy-done.1
  13.4 15.7 %all-gather = bf16[1,512,512]{2,1,0:T(8,128)(2,1)S(1)} all-gather(bf16[1,128,512]{2,1,0:T(8,128)(2,1)S(1)} %copy-done.1), channel_id=2, replica_groups=mesh['section'=4,'cp'=4,'tp'=2] {'cp'}, dimensions={1}, use_global_device_ids=true | all-gather | bytes 655360 | tf_op jit(solution)/shard_map/all_gather | solution.py:123
  29.1 0.2 tile.4
  29.3 0.0 copy-start.2
  29.4 0.8 %copy-done.2 = bf16[1,128,512]{2,1,0:T(8,128)(2,1)S(1)} copy-done((bf16[1,128,512]{2,1,0:T(8,128)(2,1)S(1)}, bf16[1,128,512]{2,1,0:T(8,128)(2,1)}, u32[]{:S(2)}) %copy-start.2) | copy-done | bytes 131096
  30.2 15.9 %all-gather.1 = bf16[1,512,512]{2,1,0:T(8,128)(2,1)S(1)} all-gather(bf16[1,128,512]{2,1,0:T(8,128)(2,1)S(1)} %copy-done.2), channel_id=3, replica_groups=mesh['section'=4,'cp'=4,'tp'=2] {'cp'}, dimensions={1}, use_global_device_ids=true | all-gather | bytes 655360 | tf_op jit(solution)/shard_map/all_gather | solution.py:124
  46.2 0.0 collective-permute-done.2.refs_0_
  46.2 0.0 collective-permute-done.3.refs_1_
  46.2 9.5 %shard_map.93 = (bf16[1,128,4096]{2,1,0:T(8,128)(2,1)}, bf16[1,128,4096]{2,1,0:T(8,128)(2,1)}, bf16[512,512]{1,0:T(8,128)(2,1)S(1)}) custom-call(bf16[1,128,2048]{2,1,0:T(8,128)(2,1)S(1)} %collective-permute-done.2.refs_0_, bf16[1,128,2048]{2,1,0:T(8,128)(2,1)S(1)} %collective-permute-done.3.refs_1_, bf16[512,512]{1,0:T(8,128)(2,1)S(1)} %bitcast.12, ...), custom_call_target="tpu_custom_call" | custom-call | flops 1610612736 | bytes 3145728 | tf_op jit(solution)/shard_map/pallas_call | solution.py:73
  55.7 2.2 %collective-permute-start.4 = (bf16[128,512]{1,0:T(8,128)(2,1)S(1)}, bf16[128,512]{1,0:T(8,128)(2,1)S(1)}, u32[]{:S(2)}, u32[]{:S(2)}) collective-permute-start(bf16[128,512]{1,0:T(8,128)(2,1)S(1)} %get-tuple-element.28), channel_id=1, source_target_pairs={{6,0},{0,2},{2,4},{4,6},{7,1},{1,3},{3,5},{5,7},{14,8},{8,10},{10,... | collective-permute-start | bytes 393224 | tf_op jit(solution)/shard_map/ppermute | solution.py:17
  57.8 2.5 %collective-permute-start.5 = (bf16[128,512]{1,0:T(8,128)(2,1)S(1)}, bf16[128,512]{1,0:T(8,128)(2,1)S(1)}, u32[]{:S(2)}, u32[]{:S(2)}) collective-permute-start(bf16[128,512]{1,0:T(8,128)(2,1)S(1)} %get-tuple-element.30), channel_id=1, source_target_pairs={{4,0},{6,2},{0,4},{2,6},{5,1},{7,3},{1,5},{3,7},{12,8},{14,10},{8,... | collective-permute-start | bytes 393224 | tf_op jit(solution)/shard_map/ppermute | solution.py:17
  60.4 0.0 collective-permute-start.6
  60.4 0.0 collective-permute-done.refs_0_
  60.4 0.0 collective-permute-done.1.refs_1_
  60.4 9.5 %shard_map.94 = (bf16[1,128,4096]{2,1,0:T(8,128)(2,1)}, bf16[1,128,4096]{2,1,0:T(8,128)(2,1)}, bf16[512,512]{1,0:T(8,128)(2,1)S(1)}) custom-call(bf16[1,128,2048]{2,1,0:T(8,128)(2,1)S(1)} %collective-permute-done.refs_0_, bf16[1,128,2048]{2,1,0:T(8,128)(2,1)S(1)} %collective-permute-done.1.refs_1_, ...), custom_call_target="tpu_custom_call", output_to_operand_aliasing={{0}: (5, {}), {1}: (6, {})} | custom-call | flops 1610612736 | bytes 3145728 | tf_op jit(solution)/shard_map/pallas_call | solution.py:73
  69.9 2.1 %collective-permute-start.7 = (bf16[128,512]{1,0:T(8,128)(2,1)S(1)}, bf16[128,512]{1,0:T(8,128)(2,1)S(1)}, u32[]{:S(2)}, u32[]{:S(2)}) collective-permute-start(bf16[128,512]{1,0:T(8,128)(2,1)S(1)} %get-tuple-element.31), channel_id=1, source_target_pairs={{6,0},{0,2},{2,4},{4,6},{7,1},{1,3},{3,5},{5,7},{14,8},{8,10},{10,... | collective-permute-start | bytes 393224 | tf_op jit(solution)/shard_map/ppermute | solution.py:17
  72.0 0.4 collective-permute-start.8
  72.4 0.0 collective-permute-done.4
  72.4 2.0 %collective-permute-start.9 = (bf16[128,512]{1,0:T(8,128)(2,1)S(1)}, bf16[128,512]{1,0:T(8,128)(2,1)S(1)}, u32[]{:S(2)}, u32[]{:S(2)}) collective-permute-start(bf16[128,512]{1,0:T(8,128)(2,1)S(1)} %get-tuple-element.32), channel_id=1, source_target_pairs={{2,0},{4,2},{6,4},{0,6},{3,1},{5,3},{7,5},{1,7},{10,8},{12,10},{14... | collective-permute-start | bytes 393224 | tf_op jit(solution)/shard_map/ppermute | solution.py:17
  74.4 0.0 collective-permute-done.5
  74.4 0.0 collective-permute-done.6
  74.4 0.1 add_convert_fusion.1
  74.5 2.3 %collective-permute-done.7 = bf16[128,512]{1,0:T(8,128)(2,1)S(1)} collective-permute-done((bf16[128,512]{1,0:T(8,128)(2,1)S(1)}, bf16[128,512]{1,0:T(8,128)(2,1)S(1)}, u32[]{:S(2)}, u32[]{:S(2)}) %collective-permute-start.7) | collective-permute-done | bytes 131104 | tf_op jit(solution)/shard_map/ppermute | solution.py:17
  76.9 2.7 %collective-permute-done.8 = bf16[128,512]{1,0:T(8,128)(2,1)S(1)} collective-permute-done((bf16[128,512]{1,0:T(8,128)(2,1)S(1)}, bf16[128,512]{1,0:T(8,128)(2,1)S(1)}, u32[]{:S(2)}, u32[]{:S(2)}) %collective-permute-start.8) | collective-permute-done | bytes 131104 | tf_op jit(solution)/shard_map/ppermute | solution.py:17
  79.6 0.0 collective-permute-done.9
  79.6 0.1 add_convert_fusion
  79.7 0.2 reshape.79
  79.9 0.4 fusion.3
  80.2 0.2 copy.20
  80.4 0.8 copy.18
  81.2 0.2 copy.21
  81.3 0.8 copy.19
  (6 shorter events, 0.1 us)
Async XLA Ops:
  0.6 5.3 %copy-start = (bf16[1,128,4096]{2,1,0:T(8,128)(2,1)S(1)}, bf16[1,128,4096]{2,1,0:T(8,128)(2,1)}, u32[]{:S(2)}) copy-start(bf16[1,128,4096]{2,1,0:T(8,128)(2,1)} %param.9) | copy-start | bytes 3145732
  3.0 43.2 %collective-permute-start.2 = (bf16[1,128,2048]{2,1,0:T(8,128)(2,1)}, bf16[1,128,2048]{2,1,0:T(8,128)(2,1)S(1)}, u32[]{:S(2)}, u32[]{:S(2)}) collective-permute-start(bf16[1,128,2048]{2,1,0:T(8,128)(2,1)} %get-tuple-element.26), channel_id=1, source_target_pairs={{24,0},{0,8},{8,16},{16,24},{25,1},{1,9},{9,17},{17,25},{26,2},{2,... | collective-permute-start | bytes 1572872 | tf_op jit(solution)/shard_map/ppermute | solution.py:17
  7.0 39.2 %collective-permute-start.3 = (bf16[1,128,2048]{2,1,0:T(8,128)(2,1)}, bf16[1,128,2048]{2,1,0:T(8,128)(2,1)S(1)}, u32[]{:S(2)}, u32[]{:S(2)}) collective-permute-start(bf16[1,128,2048]{2,1,0:T(8,128)(2,1)} %get-tuple-element.24), channel_id=1, source_target_pairs={{8,0},{16,8},{24,16},{0,24},{9,1},{17,9},{25,17},{1,25},{10,2},{18... | collective-permute-start | bytes 1572872 | tf_op jit(solution)/shard_map/ppermute | solution.py:17
  8.0 52.4 %collective-permute-start = (bf16[1,128,2048]{2,1,0:T(8,128)(2,1)}, bf16[1,128,2048]{2,1,0:T(8,128)(2,1)S(1)}, u32[]{:S(2)}, u32[]{:S(2)}) collective-permute-start(bf16[1,128,2048]{2,1,0:T(8,128)(2,1)} %get-tuple-element.27), channel_id=1, source_target_pairs={{24,0},{0,8},{8,16},{16,24},{25,1},{1,9},{9,17},{17,25},{26,2},{2,... | collective-permute-start | bytes 1572872 | tf_op jit(solution)/shard_map/ppermute | solution.py:17
  9.0 51.3 %collective-permute-start.1 = (bf16[1,128,2048]{2,1,0:T(8,128)(2,1)}, bf16[1,128,2048]{2,1,0:T(8,128)(2,1)S(1)}, u32[]{:S(2)}, u32[]{:S(2)}) collective-permute-start(bf16[1,128,2048]{2,1,0:T(8,128)(2,1)} %get-tuple-element.25), channel_id=1, source_target_pairs={{8,0},{16,8},{24,16},{0,24},{9,1},{17,9},{25,17},{1,25},{10,2},{18... | collective-permute-start | bytes 1572872 | tf_op jit(solution)/shard_map/ppermute | solution.py:17
  10.9 0.7 copy-start.3
  11.6 0.7 copy-start.4
  12.5 0.9 %copy-start.1 = (bf16[1,128,512]{2,1,0:T(8,128)(2,1)S(1)}, bf16[1,128,512]{2,1,0:T(8,128)(2,1)}, u32[]{:S(2)}) copy-start(bf16[1,128,512]{2,1,0:T(8,128)(2,1)} %param.7) | copy-start | bytes 393220
  29.3 0.9 %copy-start.2 = (bf16[1,128,512]{2,1,0:T(8,128)(2,1)S(1)}, bf16[1,128,512]{2,1,0:T(8,128)(2,1)}, u32[]{:S(2)}) copy-start(bf16[1,128,512]{2,1,0:T(8,128)(2,1)} %param.8) | copy-start | bytes 393220
  55.7 16.7 %collective-permute-start.4 = (bf16[128,512]{1,0:T(8,128)(2,1)S(1)}, bf16[128,512]{1,0:T(8,128)(2,1)S(1)}, u32[]{:S(2)}, u32[]{:S(2)}) collective-permute-start(bf16[128,512]{1,0:T(8,128)(2,1)S(1)} %get-tuple-element.28), channel_id=1, source_target_pairs={{6,0},{0,2},{2,4},{4,6},{7,1},{1,3},{3,5},{5,7},{14,8},{8,10},{10,... | collective-permute-start | bytes 393224 | tf_op jit(solution)/shard_map/ppermute | solution.py:17
  57.8 16.6 %collective-permute-start.5 = (bf16[128,512]{1,0:T(8,128)(2,1)S(1)}, bf16[128,512]{1,0:T(8,128)(2,1)S(1)}, u32[]{:S(2)}, u32[]{:S(2)}) collective-permute-start(bf16[128,512]{1,0:T(8,128)(2,1)S(1)} %get-tuple-element.30), channel_id=1, source_target_pairs={{4,0},{6,2},{0,4},{2,6},{5,1},{7,3},{1,5},{3,7},{12,8},{14,10},{8,... | collective-permute-start | bytes 393224 | tf_op jit(solution)/shard_map/ppermute | solution.py:17
  60.4 14.1 %collective-permute-start.6 = (bf16[128,512]{1,0:T(8,128)(2,1)S(1)}, bf16[128,512]{1,0:T(8,128)(2,1)S(1)}, u32[]{:S(2)}, u32[]{:S(2)}) collective-permute-start(bf16[128,512]{1,0:T(8,128)(2,1)S(1)} %get-tuple-element.29), channel_id=1, source_target_pairs={{2,0},{4,2},{6,4},{0,6},{3,1},{5,3},{7,5},{1,7},{10,8},{12,10},{14... | collective-permute-start | bytes 393224 | tf_op jit(solution)/shard_map/ppermute | solution.py:17
  69.9 6.9 %collective-permute-start.7 = (bf16[128,512]{1,0:T(8,128)(2,1)S(1)}, bf16[128,512]{1,0:T(8,128)(2,1)S(1)}, u32[]{:S(2)}, u32[]{:S(2)}) collective-permute-start(bf16[128,512]{1,0:T(8,128)(2,1)S(1)} %get-tuple-element.31), channel_id=1, source_target_pairs={{6,0},{0,2},{2,4},{4,6},{7,1},{1,3},{3,5},{5,7},{14,8},{8,10},{10,... | collective-permute-start | bytes 393224 | tf_op jit(solution)/shard_map/ppermute | solution.py:17
  72.0 7.6 %collective-permute-start.8 = (bf16[128,512]{1,0:T(8,128)(2,1)S(1)}, bf16[128,512]{1,0:T(8,128)(2,1)S(1)}, u32[]{:S(2)}, u32[]{:S(2)}) collective-permute-start(bf16[128,512]{1,0:T(8,128)(2,1)S(1)} %get-tuple-element.33), channel_id=1, source_target_pairs={{4,0},{6,2},{0,4},{2,6},{5,1},{7,3},{1,5},{3,7},{12,8},{14,10},{8,... | collective-permute-start | bytes 393224 | tf_op jit(solution)/shard_map/ppermute | solution.py:17
  72.4 7.2 %collective-permute-start.9 = (bf16[128,512]{1,0:T(8,128)(2,1)S(1)}, bf16[128,512]{1,0:T(8,128)(2,1)S(1)}, u32[]{:S(2)}, u32[]{:S(2)}) collective-permute-start(bf16[128,512]{1,0:T(8,128)(2,1)S(1)} %get-tuple-element.32), channel_id=1, source_target_pairs={{2,0},{4,2},{6,4},{0,6},{3,1},{5,3},{7,5},{1,7},{10,8},{12,10},{14... | collective-permute-start | bytes 393224 | tf_op jit(solution)/shard_map/ppermute | solution.py:17
